TPU v7x, 32 devices: a whole 2x2x4 slice. The times are simulated.
32 devices in a mesh: gx: 2 (over x), gy: 4 (over y, core), gz: 4 (over z).
Axes of the slice: x: 2, y: 2, z: 4, core: 2. Of those that a mesh axis runs over, the one named last changes fastest.
Arguments:
- rhs: float32 [8, 8, 2, 16, 512], P(None, None, 'gx', 'gy', 'gz'), as said below
- blocks: bfloat16 [7, 8, 8, 2, 16, 512], P(None, None, None, 'gx', 'gy', 'gz'), as said below
Outputs:
- basis: float32 [4, 8, 8, 2, 16, 512], P(None, None, None, 'gx', 'gy', 'gz')
- hess: float32 [4, 8, 3, 8], replicated
Inputs may be any that keep to these rules, and one draw needn't show every extreme that they name: `rhs`: each cell's value is a random draw times a positive scale that varies smoothly over the grid. The operator couples each cell only to itself and its six face neighbours; its blocks are full and the block Krylov spaces keep full rank.
All inputs are finite; a program needn't handle non-finite values.
Results may differ from a plain program's by a relative error of at most 0.001.
Values sent between devices are 32-bit elements; how exact they have to be, the bound alone decides.
A program may use at most 64 MiB of HBM per device.

v0:
```python
import jax
import jax.numpy as jnp
from jax import lax
from jax.sharding import PartitionSpec as P

RHS = 8
ITERS = 3
HIGH = lax.Precision.HIGHEST


def with_halo(block, sides, width):
    for axis, dim in sides:
        count = lax.axis_size(axis)
        forward = [(i, i + 1) for i in range(count - 1)]
        backward = [(target, source) for source, target in forward]
        low = lax.ppermute(
            lax.slice_in_dim(block, block.shape[dim] - width, None, axis=dim), axis, forward
        )
        high = lax.ppermute(lax.slice_in_dim(block, 0, width, axis=dim), axis, backward)
        block = jnp.concatenate([low, block, high], axis=dim)
    return block


def couple(padded, blocks):
    views = [
        padded[:, :, 1:-1, 1:-1, 1:-1],
        padded[:, :, 2:, 1:-1, 1:-1],
        padded[:, :, :-2, 1:-1, 1:-1],
        padded[:, :, 1:-1, 2:, 1:-1],
        padded[:, :, 1:-1, :-2, 1:-1],
        padded[:, :, 1:-1, 1:-1, 2:],
        padded[:, :, 1:-1, 1:-1, :-2],
    ]
    total = jnp.zeros(views[0].shape, jnp.float32)
    for k in range(7):
        for j in range(views[0].shape[0]):
            column = blocks[k, :, j].astype(jnp.float32)
            total = total + column[:, None] * views[k][j][None]
    return total


def stencil(field, blocks):
    padded = with_halo(field, (("gx", 2), ("gy", 3), ("gz", 4)), 1)
    return couple(padded, blocks)


def pair(first, second):
    return jnp.einsum("arxyz,asxyz->rs", first, second, precision=HIGH)


def mix(field, matrix):
    return jnp.einsum("asxyz,sr->arxyz", field, matrix, precision=HIGH)


def normalizer(gram, eye):
    lower = jnp.linalg.cholesky(gram)
    inverse = lax.linalg.triangular_solve(lower, eye, left_side=True, lower=True)
    return (inverse.T, lower.T)


def shards(rhs, blocks):
    eye = jnp.eye(RHS, dtype=jnp.float32)
    hess = jnp.zeros((ITERS + 1, RHS, ITERS, RHS), jnp.float32)
    first_pair = None
    raw_image = stencil(rhs, blocks)
    gram_start, cross, square = lax.psum(
        (pair(rhs, rhs), pair(rhs, raw_image), pair(raw_image, raw_image)), ("gx", "gy", "gz")
    )
    scale, upper = normalizer(gram_start, eye)
    basis = [mix(rhs, scale)]
    images = [mix(raw_image, scale)]
    first_coeff = jnp.dot(jnp.dot(scale.T, cross, precision=HIGH), scale, precision=HIGH)
    first_gram = jnp.dot(jnp.dot(scale.T, square, precision=HIGH), scale, precision=HIGH)
    first_pair = (first_coeff, first_gram)
    for step in range(ITERS):
        image = images[step]
        if step == 0 and first_pair is not None:
            coeffs = [first_pair[0]]
            gram = first_pair[1]
        else:
            stacked = jnp.stack(basis + [image])
            partial_sums = jnp.einsum("karxyz,asxyz->krs", stacked, image, precision=HIGH)
            summed = lax.psum(partial_sums, ("gx", "gy", "gz"))
            coeffs = [summed[index] for index in range(len(basis))]
            gram = summed[len(basis)]
        rest = image
        for vector, coeff in zip(basis, coeffs):
            gram = gram - jnp.dot(coeff.T, coeff, precision=HIGH)
            rest = rest - mix(vector, coeff)
        scale, upper = normalizer(gram, eye)
        fresh = mix(rest, scale)
        basis.append(fresh)
        for index, coeff in enumerate(coeffs):
            hess = hess.at[index, :, step, :].set(coeff)
        hess = hess.at[step + 1, :, step, :].set(upper)
        if step + 1 < ITERS:
            images.append(stencil(fresh, blocks))
    return (jnp.stack(basis), hess)


def solution(mesh):
    placed = (P(None, None, "gx", "gy", "gz"), P(None, None, None, "gx", "gy", "gz"))
    return jax.shard_map(
        shards,
        mesh=mesh,
        in_specs=placed,
        out_specs=(P(None, None, None, "gx", "gy", "gz"), P()),
        check_vma=False,
    )
```

profile of v0, /device:TPU:0, one launch (start us, length us, event | category | flops | bytes accessed | tf_op | source)
XLA Modules:
  0.0 246.0 jit_solution(17078392354189909345)
XLA Ops:
  0.6 1.0 copy.203
  1.6 4.9 %collective-permute-start.1 = (f32[8,8,1,4,128]{4,1,3,2,0:T(8,128)S(1)}, f32[8,8,1,4,128]{4,1,3,2,0:T(8,128)S(1)}, u32[]{:S(2)}, u32[]{:S(2)}) collective-permute-start(f32[8,8,1,4,128]{4,1,3,2,0:T(8,128)S(1)} %copy.203), channel_id=1, source_target_pairs={{0,16},{1,17},{2,18},{3,19},{4,20},{5,21},{6,22},{7,23},{8,24},{9,... | collective-permute-start | bytes 393224 | tf_op jit(solution)/shard_map/ppermute | solution.py:16
  6.5 1.3 collective-permute-start
  7.8 0.9 bitcast_convert_fusion.53
  10.2 3.1 %collective-permute-done = f32[8,8,1,4,128]{4,1,3,2,0:T(8,128)S(1)} collective-permute-done((f32[8,8,1,4,128]{4,1,3,2,0:T(8,128)S(1)}, f32[8,8,1,4,128]{4,1,3,2,0:T(8,128)S(1)}, u32[]{:S(2)}, u32[]{:S(2)}) %collective-permute-start) | collective-permute-done | bytes 131104 | tf_op jit(solution)/shard_map/ppermute | solution.py:19
  13.4 1.3 collective-permute-start.2
  14.7 3.0 %collective-permute-start.3 = (f32[8,8,3,1,128]{4,1,3,2,0:T(8,128)S(1)}, f32[8,8,3,1,128]{4,1,3,2,0:T(8,128)S(1)}, u32[]{:S(2)}, u32[]{:S(2)}) collective-permute-start(f32[8,8,3,1,128]{4,1,3,2,0:T(8,128)S(1)} %get-tuple-element.285), channel_id=1, source_target_pairs={{0,4},{4,8},{8,12},{1,5},{5,9},{9,13},{2,6},{6,10},{10,14},{3,7},{... | collective-permute-start | bytes 294920 | tf_op jit(solution)/shard_map/ppermute | solution.py:16
  18.9 0.9 copy.278
  19.8 3.5 %collective-permute-start.5 = (f32[8,8,3,6,1]{1,0,4,3,2:T(8,128)S(1)}, f32[8,8,3,6,1]{1,0,4,3,2:T(8,128)S(1)}, u32[]{:S(2)}, u32[]{:S(2)}) collective-permute-start(f32[8,8,3,6,1]{1,0,4,3,2:T(8,128)S(1)} %copy.278), channel_id=1, source_target_pairs={{0,1},{1,2},{2,3},{4,5},{5,6},{6,7},{8,9},{9,10},{10,11},{12,13},{... | collective-permute-start | bytes 13832 | tf_op jit(solution)/shard_map/ppermute | solution.py:16
  24.2 1.3 collective-permute-start.4
  25.6 0.9 copy.209
  26.7 4.0 %collective-permute-done.4 = f32[8,8,3,6,1]{1,0,4,3,2:T(8,128)S(1)} collective-permute-done((f32[8,8,3,6,1]{1,0,4,3,2:T(8,128)S(1)}, f32[8,8,3,6,1]{1,0,4,3,2:T(8,128)S(1)}, u32[]{:S(2)}, u32[]{:S(2)}) %collective-permute-start.4) | collective-permute-done | bytes 4640 | tf_op jit(solution)/shard_map/ppermute | solution.py:19
  30.7 0.9 copy.207
  31.8 1.0 multiply_add_fusion.2
  33.6 41.6 %all-reduce.1 = (f32[8,8]{0,1:T(8,128)S(1)}, f32[8,8]{1,0:T(8,128)S(1)}, f32[8,8]{0,1:T(8,128)S(1)}) all-reduce(f32[8,8]{0,1:T(8,128)S(1)} %convolution_bitcast_fusion.13, f32[8,8]{1,0:T(8,128)S(1)} %convolution_bitcast_fusion.12, f32[8,8]{0,1:T(8,128)S(1)} %convolution_bitcast_fusion.11), channel_id=1, replica_groups=mesh['gx'=2,'gy'=4,'gz'=4] {'gx','gy','gz'}, use_global_device_ids=true, to_apply=%region_0.0 | all-reduce | flops 192 | bytes 1536 | tf_op jit(solution)/shard_map/psum | solution.py:66
  83.0 1.3 collective-permute-start.6
  84.3 4.6 %collective-permute-start.7 = (f32[8,8,1,4,128]{4,1,3,0,2:T(8,128)S(1)}, f32[8,8,1,4,128]{4,1,3,0,2:T(8,128)S(1)}, u32[]{:S(2)}, u32[]{:S(2)}) collective-permute-start(f32[8,8,1,4,128]{4,1,3,0,2:T(8,128)S(1)} %bitcast.786), channel_id=1, source_target_pairs={{0,16},{1,17},{2,18},{3,19},{4,20},{5,21},{6,22},{7,23},{8,24},{9,... | collective-permute-start | bytes 393224 | tf_op jit(solution)/shard_map/ppermute | solution.py:16
  90.8 2.8 %and_reduce_fusion = (pred[]{:T(512)}, pred[]{:T(512)}) fusion(s32[4]{0:T(128)S(1)} %copy-done.3, s32[1]{0:T(128)} %constant.288.clone.1, s32[1]{0:T(128)} %get-tuple-element.366, s32[1]{0:T(128)} %get-tuple-element.365, s32[1]{0:T(128)} %slice.1472, s32[1]{0:T(128)S(1)} %bitcast.825), kind=kLoop, calls=%fused_computation.849 | loop fusion | flops 54 | bytes 38 | tf_op jit(solution)/shard_map/reduce.18
  93.7 1.3 collective-permute-start.8
  95.0 3.0 %collective-permute-start.9 = (f32[8,8,3,1,128]{4,1,3,0,2:T(8,128)S(1)}, f32[8,8,3,1,128]{4,1,3,0,2:T(8,128)S(1)}, u32[]{:S(2)}, u32[]{:S(2)}) collective-permute-start(f32[8,8,3,1,128]{4,1,3,0,2:T(8,128)S(1)} %get-tuple-element.283), channel_id=1, source_target_pairs={{0,4},{4,8},{8,12},{1,5},{5,9},{9,13},{2,6},{6,10},{10,14},{3,7},{... | collective-permute-start | bytes 294920 | tf_op jit(solution)/shard_map/ppermute | solution.py:16
  99.2 0.9 copy.218
  100.1 2.2 collective-permute-start.11
  103.2 1.3 collective-permute-start.10
  104.6 0.9 copy.219
  105.7 3.7 %collective-permute-done.10 = f32[8,8,3,6,1]{1,0,4,3,2:T(8,128)S(1)} collective-permute-done((f32[8,8,3,6,1]{1,0,4,3,2:T(8,128)S(1)}, f32[8,8,3,6,1]{1,0,4,3,2:T(8,128)S(1)}, u32[]{:S(2)}, u32[]{:S(2)}) %collective-permute-start.10) | collective-permute-done | bytes 4640 | tf_op jit(solution)/shard_map/ppermute | solution.py:19
  109.4 0.9 copy.217
  110.6 1.1 multiply_add_fusion.1
  111.7 1.6 convolution_bitcast_fusion.7
  113.3 42.8 %psum.38 = f32[3,8,8]{2,1,0:T(8,128)S(1)} all-reduce(f32[3,8,8]{2,1,0:T(8,128)S(1)} %convolution_bitcast_fusion.7), channel_id=1, replica_groups=mesh['gx'=2,'gy'=4,'gz'=4] {'gx','gy','gz'}, use_global_device_ids=true, to_apply=%region_5.8 | all-reduce | flops 192 | bytes 1536 | tf_op jit(solution)/shard_map/psum | solution.py:83
  159.8 1.3 fusion.3
  161.4 1.3 collective-permute-start.12
  162.7 4.6 %collective-permute-start.13 = (f32[8,8,1,4,128]{4,1,3,0,2:T(8,128)S(1)}, f32[8,8,1,4,128]{4,1,3,0,2:T(8,128)S(1)}, u32[]{:S(2)}, u32[]{:S(2)}) collective-permute-start(f32[8,8,1,4,128]{4,1,3,0,2:T(8,128)S(1)} %bitcast.803), channel_id=1, source_target_pairs={{0,16},{1,17},{2,18},{3,19},{4,20},{5,21},{6,22},{7,23},{8,24},{9,... | collective-permute-start | bytes 393224 | tf_op jit(solution)/shard_map/ppermute | solution.py:16
  167.3 1.3 fusion.499
  168.7 1.1 collective-permute-done.13
  169.8 1.3 collective-permute-start.14
  171.1 3.0 %collective-permute-start.15 = (f32[8,8,3,1,128]{4,1,3,0,2:T(8,128)S(1)}, f32[8,8,3,1,128]{4,1,3,0,2:T(8,128)S(1)}, u32[]{:S(2)}, u32[]{:S(2)}) collective-permute-start(f32[8,8,3,1,128]{4,1,3,0,2:T(8,128)S(1)} %get-tuple-element.281), channel_id=1, source_target_pairs={{0,4},{4,8},{8,12},{1,5},{5,9},{9,13},{2,6},{6,10},{10,14},{3,7},{... | collective-permute-start | bytes 294920 | tf_op jit(solution)/shard_map/ppermute | solution.py:16
  175.3 0.9 copy.230
  176.2 2.2 collective-permute-start.17
  179.3 1.3 collective-permute-start.16
  180.7 0.9 copy.231
  181.8 3.7 %collective-permute-done.16 = f32[8,8,3,6,1]{1,0,4,3,2:T(8,128)S(1)} collective-permute-done((f32[8,8,3,6,1]{1,0,4,3,2:T(8,128)S(1)}, f32[8,8,3,6,1]{1,0,4,3,2:T(8,128)S(1)}, u32[]{:S(2)}, u32[]{:S(2)}) %collective-permute-start.16) | collective-permute-done | bytes 4640 | tf_op jit(solution)/shard_map/ppermute | solution.py:19
  185.5 0.9 copy.229
  186.7 1.0 multiply_add_fusion
  187.8 1.6 convolution_bitcast_fusion.6
  189.4 44.9 %psum.39 = f32[4,8,8]{2,1,0:T(8,128)S(1)} all-reduce(f32[4,8,8]{2,1,0:T(8,128)S(1)} %convolution_bitcast_fusion.6), channel_id=1, replica_groups=mesh['gx'=2,'gy'=4,'gz'=4] {'gx','gy','gz'}, use_global_device_ids=true, to_apply=%region_6.9 | all-reduce | flops 256 | bytes 2048 | tf_op jit(solution)/shard_map/psum | solution.py:83
  238.6 1.1 fusion.7
  240.0 0.9 copy.245
  240.9 3.3 %fusion.498 = f32[4,8,3,8]{3,1,2,0:T(8,128)} fusion(f32[4,8,3,8]{3,1,2,0:T(8,128)} %copy-done.2, s32[]{:T(128)} %bitcast.379, s32[]{:T(128)} %bitcast.380, f32[4,8,8]{2,1,0:T(8,128)S(1)} %psum.39, pred[]{:T(512)} %get-tuple-element.118), kind=kLoop, calls=%fused_computation.797 | loop fusion | flops 64 | bytes 9984 | tf_op jit(solution)/shard_map/scatter | solution.py:94
  (149 shorter events, 30.1 us)
Async XLA Ops:
  0.6 8.1 %copy-start.1 = (bf16[7,8,8,1,4,128]{5,4,3,2,1,0:T(4,128)(2,1)S(1)}, bf16[7,8,8,1,4,128]{5,4,3,2,1,0:T(4,128)(2,1)}, u32[]{:S(2)}) copy-start(bf16[7,8,8,1,4,128]{5,4,3,2,1,0:T(4,128)(2,1)} %param.24) | copy-start | bytes 1376260
  1.6 8.5 %collective-permute-start.1 = (f32[8,8,1,4,128]{4,1,3,2,0:T(8,128)S(1)}, f32[8,8,1,4,128]{4,1,3,2,0:T(8,128)S(1)}, u32[]{:S(2)}, u32[]{:S(2)}) collective-permute-start(f32[8,8,1,4,128]{4,1,3,2,0:T(8,128)S(1)} %copy.203), channel_id=1, source_target_pairs={{0,16},{1,17},{2,18},{3,19},{4,20},{5,21},{6,22},{7,23},{8,24},{9,... | collective-permute-start | bytes 393224 | tf_op jit(solution)/shard_map/ppermute | solution.py:16
  6.5 6.9 %collective-permute-start = (f32[8,8,1,4,128]{4,1,3,2,0:T(8,128)S(1)}, f32[8,8,1,4,128]{4,1,3,2,0:T(8,128)S(1)}, u32[]{:S(2)}, u32[]{:S(2)}) collective-permute-start(f32[8,8,1,4,128]{4,1,3,2,0:T(8,128)S(1)} %copy.203), channel_id=1, source_target_pairs={{16,0},{17,1},{18,2},{19,3},{20,4},{21,5},{22,6},{23,7},{24,8},{25... | collective-permute-start | bytes 393224 | tf_op jit(solution)/shard_map/ppermute | solution.py:19
  8.8 0.9 copy-start
  13.4 4.4 %collective-permute-start.2 = (f32[8,8,3,1,128]{4,1,3,2,0:T(8,128)S(1)}, f32[8,8,3,1,128]{4,1,3,2,0:T(8,128)S(1)}, u32[]{:S(2)}, u32[]{:S(2)}) collective-permute-start(f32[8,8,3,1,128]{4,1,3,2,0:T(8,128)S(1)} %get-tuple-element.286), channel_id=1, source_target_pairs={{4,0},{8,4},{12,8},{5,1},{9,5},{13,9},{6,2},{10,6},{14,10},{7,3},{... | collective-permute-start | bytes 294920 | tf_op jit(solution)/shard_map/ppermute | solution.py:19
  14.7 4.0 %collective-permute-start.3 = (f32[8,8,3,1,128]{4,1,3,2,0:T(8,128)S(1)}, f32[8,8,3,1,128]{4,1,3,2,0:T(8,128)S(1)}, u32[]{:S(2)}, u32[]{:S(2)}) collective-permute-start(f32[8,8,3,1,128]{4,1,3,2,0:T(8,128)S(1)} %get-tuple-element.285), channel_id=1, source_target_pairs={{0,4},{4,8},{8,12},{1,5},{5,9},{9,13},{2,6},{6,10},{10,14},{3,7},{... | collective-permute-start | bytes 294920 | tf_op jit(solution)/shard_map/ppermute | solution.py:16
  19.8 5.7 %collective-permute-start.5 = (f32[8,8,3,6,1]{1,0,4,3,2:T(8,128)S(1)}, f32[8,8,3,6,1]{1,0,4,3,2:T(8,128)S(1)}, u32[]{:S(2)}, u32[]{:S(2)}) collective-permute-start(f32[8,8,3,6,1]{1,0,4,3,2:T(8,128)S(1)} %copy.278), channel_id=1, source_target_pairs={{0,1},{1,2},{2,3},{4,5},{5,6},{6,7},{8,9},{9,10},{10,11},{12,13},{... | collective-permute-start | bytes 13832 | tf_op jit(solution)/shard_map/ppermute | solution.py:16
  24.2 6.5 %collective-permute-start.4 = (f32[8,8,3,6,1]{1,0,4,3,2:T(8,128)S(1)}, f32[8,8,3,6,1]{1,0,4,3,2:T(8,128)S(1)}, u32[]{:S(2)}, u32[]{:S(2)}) collective-permute-start(f32[8,8,3,6,1]{1,0,4,3,2:T(8,128)S(1)} %copy.277), channel_id=1, source_target_pairs={{1,0},{2,1},{3,2},{5,4},{6,5},{7,6},{9,8},{10,9},{11,10},{13,12},{... | collective-permute-start | bytes 13832 | tf_op jit(solution)/shard_map/ppermute | solution.py:19
  83.0 10.6 %collective-permute-start.6 = (f32[8,8,1,4,128]{4,1,3,0,2:T(8,128)S(1)}, f32[8,8,1,4,128]{4,1,3,0,2:T(8,128)S(1)}, u32[]{:S(2)}, u32[]{:S(2)}) collective-permute-start(f32[8,8,1,4,128]{4,1,3,0,2:T(8,128)S(1)} %bitcast.785), channel_id=1, source_target_pairs={{16,0},{17,1},{18,2},{19,3},{20,4},{21,5},{22,6},{23,7},{24,8},{25... | collective-permute-start | bytes 393224 | tf_op jit(solution)/shard_map/ppermute | solution.py:19
  84.3 9.3 %collective-permute-start.7 = (f32[8,8,1,4,128]{4,1,3,0,2:T(8,128)S(1)}, f32[8,8,1,4,128]{4,1,3,0,2:T(8,128)S(1)}, u32[]{:S(2)}, u32[]{:S(2)}) collective-permute-start(f32[8,8,1,4,128]{4,1,3,0,2:T(8,128)S(1)} %bitcast.786), channel_id=1, source_target_pairs={{0,16},{1,17},{2,18},{3,19},{4,20},{5,21},{6,22},{7,23},{8,24},{9,... | collective-permute-start | bytes 393224 | tf_op jit(solution)/shard_map/ppermute | solution.py:16
  90.1 0.7 copy-start.3
  93.7 4.4 %collective-permute-start.8 = (f32[8,8,3,1,128]{4,1,3,0,2:T(8,128)S(1)}, f32[8,8,3,1,128]{4,1,3,0,2:T(8,128)S(1)}, u32[]{:S(2)}, u32[]{:S(2)}) collective-permute-start(f32[8,8,3,1,128]{4,1,3,0,2:T(8,128)S(1)} %get-tuple-element.284), channel_id=1, source_target_pairs={{4,0},{8,4},{12,8},{5,1},{9,5},{13,9},{6,2},{10,6},{14,10},{7,3},{... | collective-permute-start | bytes 294920 | tf_op jit(solution)/shard_map/ppermute | solution.py:19
  95.0 4.0 %collective-permute-start.9 = (f32[8,8,3,1,128]{4,1,3,0,2:T(8,128)S(1)}, f32[8,8,3,1,128]{4,1,3,0,2:T(8,128)S(1)}, u32[]{:S(2)}, u32[]{:S(2)}) collective-permute-start(f32[8,8,3,1,128]{4,1,3,0,2:T(8,128)S(1)} %get-tuple-element.283), channel_id=1, source_target_pairs={{0,4},{4,8},{8,12},{1,5},{5,9},{9,13},{2,6},{6,10},{10,14},{3,7},{... | collective-permute-start | bytes 294920 | tf_op jit(solution)/shard_map/ppermute | solution.py:16
  100.1 4.5 %collective-permute-start.11 = (f32[8,8,3,6,1]{1,0,4,3,2:T(8,128)S(1)}, f32[8,8,3,6,1]{1,0,4,3,2:T(8,128)S(1)}, u32[]{:S(2)}, u32[]{:S(2)}) collective-permute-start(f32[8,8,3,6,1]{1,0,4,3,2:T(8,128)S(1)} %copy.218), channel_id=1, source_target_pairs={{0,1},{1,2},{2,3},{4,5},{5,6},{6,7},{8,9},{9,10},{10,11},{12,13},{... | collective-permute-start | bytes 13832 | tf_op jit(solution)/shard_map/ppermute | solution.py:16
  103.2 6.2 %collective-permute-start.10 = (f32[8,8,3,6,1]{1,0,4,3,2:T(8,128)S(1)}, f32[8,8,3,6,1]{1,0,4,3,2:T(8,128)S(1)}, u32[]{:S(2)}, u32[]{:S(2)}) collective-permute-start(f32[8,8,3,6,1]{1,0,4,3,2:T(8,128)S(1)} %copy.216), channel_id=1, source_target_pairs={{1,0},{2,1},{3,2},{5,4},{6,5},{7,6},{9,8},{10,9},{11,10},{13,12},{... | collective-permute-start | bytes 13832 | tf_op jit(solution)/shard_map/ppermute | solution.py:19
  161.4 7.3 %collective-permute-start.12 = (f32[8,8,1,4,128]{4,1,3,0,2:T(8,128)S(1)}, f32[8,8,1,4,128]{4,1,3,0,2:T(8,128)S(1)}, u32[]{:S(2)}, u32[]{:S(2)}) collective-permute-start(f32[8,8,1,4,128]{4,1,3,0,2:T(8,128)S(1)} %bitcast.802), channel_id=1, source_target_pairs={{16,0},{17,1},{18,2},{19,3},{20,4},{21,5},{22,6},{23,7},{24,8},{25... | collective-permute-start | bytes 393224 | tf_op jit(solution)/shard_map/ppermute | solution.py:19
  162.7 7.1 %collective-permute-start.13 = (f32[8,8,1,4,128]{4,1,3,0,2:T(8,128)S(1)}, f32[8,8,1,4,128]{4,1,3,0,2:T(8,128)S(1)}, u32[]{:S(2)}, u32[]{:S(2)}) collective-permute-start(f32[8,8,1,4,128]{4,1,3,0,2:T(8,128)S(1)} %bitcast.803), channel_id=1, source_target_pairs={{0,16},{1,17},{2,18},{3,19},{4,20},{5,21},{6,22},{7,23},{8,24},{9,... | collective-permute-start | bytes 393224 | tf_op jit(solution)/shard_map/ppermute | solution.py:16
  169.8 4.4 %collective-permute-start.14 = (f32[8,8,3,1,128]{4,1,3,0,2:T(8,128)S(1)}, f32[8,8,3,1,128]{4,1,3,0,2:T(8,128)S(1)}, u32[]{:S(2)}, u32[]{:S(2)}) collective-permute-start(f32[8,8,3,1,128]{4,1,3,0,2:T(8,128)S(1)} %get-tuple-element.282), channel_id=1, source_target_pairs={{4,0},{8,4},{12,8},{5,1},{9,5},{13,9},{6,2},{10,6},{14,10},{7,3},{... | collective-permute-start | bytes 294920 | tf_op jit(solution)/shard_map/ppermute | solution.py:19
  171.1 4.0 %collective-permute-start.15 = (f32[8,8,3,1,128]{4,1,3,0,2:T(8,128)S(1)}, f32[8,8,3,1,128]{4,1,3,0,2:T(8,128)S(1)}, u32[]{:S(2)}, u32[]{:S(2)}) collective-permute-start(f32[8,8,3,1,128]{4,1,3,0,2:T(8,128)S(1)} %get-tuple-element.281), channel_id=1, source_target_pairs={{0,4},{4,8},{8,12},{1,5},{5,9},{9,13},{2,6},{6,10},{10,14},{3,7},{... | collective-permute-start | bytes 294920 | tf_op jit(solution)/shard_map/ppermute | solution.py:16
  174.1 0.9 copy-start.2
  176.2 4.5 %collective-permute-start.17 = (f32[8,8,3,6,1]{1,0,4,3,2:T(8,128)S(1)}, f32[8,8,3,6,1]{1,0,4,3,2:T(8,128)S(1)}, u32[]{:S(2)}, u32[]{:S(2)}) collective-permute-start(f32[8,8,3,6,1]{1,0,4,3,2:T(8,128)S(1)} %copy.230), channel_id=1, source_target_pairs={{0,1},{1,2},{2,3},{4,5},{5,6},{6,7},{8,9},{9,10},{10,11},{12,13},{... | collective-permute-start | bytes 13832 | tf_op jit(solution)/shard_map/ppermute | solution.py:16
  179.3 6.2 %collective-permute-start.16 = (f32[8,8,3,6,1]{1,0,4,3,2:T(8,128)S(1)}, f32[8,8,3,6,1]{1,0,4,3,2:T(8,128)S(1)}, u32[]{:S(2)}, u32[]{:S(2)}) collective-permute-start(f32[8,8,3,6,1]{1,0,4,3,2:T(8,128)S(1)} %copy.228), channel_id=1, source_target_pairs={{1,0},{2,1},{3,2},{5,4},{6,5},{7,6},{9,8},{10,9},{11,10},{13,12},{... | collective-permute-start | bytes 13832 | tf_op jit(solution)/shard_map/ppermute | solution.py:19
where the time goes:
time: 247 us; the launch traced here: 246 us
  blocking collectives  129 us (52%)
  starting transfers between devices  42.5 us (17%)
  other arithmetic  23.9 us (10%)
  local copies, waits for them, and re-layouts  18.8 us (8%)
  waiting for transfers between devices  18.3 us (7%)
  matrix products  11.8 us (5%)
    psum x2, blocking collectives, shards(): summed = lax.psum(partial_sums, ('gx', 'gy', 'gz'))  87.7 us
    psum x1, blocking collectives, shards(): lax.psum((pair(rhs, rhs), pair(rhs, raw_image), pair(raw_image, raw_image...  41.6 us
    ppermute x9, starting transfers between devices, with_halo(): lax.ppermute(lax.slice_in_dim(block, block.shape[dim] - width, None, axis...  30.9 us
    ppermute x9, waiting for transfers between devices, with_halo(): lax.ppermute(lax.slice_in_dim(block, 0, width, axis=dim), axis, backward)  14.6 us
    ppermute x9, starting transfers between devices, with_halo(): lax.ppermute(lax.slice_in_dim(block, 0, width, axis=dim), axis, backward)  11.6 us
    another operation x12, other arithmetic, normalizer(): lower = jnp.linalg.cholesky(gram)  5.63 us
    unnamed x14, local copies, waits for them, and re-layouts  5.27 us
    dot_general x11, matrix products, mix(): return jnp.einsum('asxyz,sr->arxyz', field, matrix, precision=HIGH)  4.97 us
  transfers between devices with their start and end apart: 18, of which 8 were waited for; matrix products, arithmetic and copies ran while one was open for 5% of the time, Pallas kernels for 0%

commit v1 on v0

--- a/solution.py
+++ b/solution.py
@@ -6,6 +6,11 @@
 RHS = 8
 ITERS = 3
 HIGH = lax.Precision.HIGHEST
+
+
+def gather_and_add(x, axis):
+    blocks = lax.all_gather(x, axis)
+    return jnp.sum(blocks, axis=0)
 
 
 def with_halo(block, sides, width):
@@ -80,7 +85,7 @@
         else:
             stacked = jnp.stack(basis + [image])
             partial_sums = jnp.einsum("karxyz,asxyz->krs", stacked, image, precision=HIGH)
-            summed = lax.psum(partial_sums, ("gx", "gy", "gz"))
+            summed = gather_and_add(partial_sums, ("gx", "gy", "gz"))
             coeffs = [summed[index] for index in range(len(basis))]
             gram = summed[len(basis)]
         rest = image

time: 247 us -> 296 us (1.20)
  blocking collectives: 129 us -> 178 us
    all_gather x0 -> x2, blocking collectives: none -> 137 us  [gather_and_add(): blocks = lax.all_gather(x, axis)]
    psum x2 -> x0, blocking collectives: 87.7 us -> none  [shards(): summed = lax.psum(partial_sums, ('gx', 'gy', 'gz'))]
  transfers between devices with their start and end apart: 18 -> 18, of which waited for: 8 -> 9; matrix products, arithmetic and copies ran while one was open for 5% -> 4% of each run, Pallas kernels for 0% -> 0%
where the time goes in v1:
time: 296 us
  blocking collectives  178 us (60%)
  starting transfers between devices  42.7 us (14%)
  other arithmetic  24 us (8%)
  local copies, waits for them, and re-layouts  18.8 us (6%)
  waiting for transfers between devices  18.6 us (6%)
  matrix products  11.8 us (4%)
    all_gather x2, blocking collectives, gather_and_add(): blocks = lax.all_gather(x, axis)  137 us
    psum x1, blocking collectives, shards(): lax.psum((pair(rhs, rhs), pair(rhs, raw_image), pair(raw_image, raw_image...  41.6 us
    ppermute x9, starting transfers between devices, with_halo(): lax.ppermute(lax.slice_in_dim(block, block.shape[dim] - width, None, axis...  31.1 us
    ppermute x9, waiting for transfers between devices, with_halo(): lax.ppermute(lax.slice_in_dim(block, 0, width, axis=dim), axis, backward)  14.7 us
    ppermute x9, starting transfers between devices, with_halo(): lax.ppermute(lax.slice_in_dim(block, 0, width, axis=dim), axis, backward)  11.6 us
  transfers between devices with their start and end apart: 18, of which 9 were waited for; matrix products, arithmetic and copies ran while one was open for 4% of the time, Pallas kernels for 0%

profile of v1, /device:TPU:0, one launch (start us, length us, event | category | flops | bytes accessed | tf_op | source)
XLA Modules:
  0.0 295.6 jit_solution(8107745335727928824)
XLA Ops:
  0.6 1.0 copy.203
  1.6 4.9 %collective-permute-start.1 = (f32[8,8,1,4,128]{4,1,3,2,0:T(8,128)S(1)}, f32[8,8,1,4,128]{4,1,3,2,0:T(8,128)S(1)}, u32[]{:S(2)}, u32[]{:S(2)}) collective-permute-start(f32[8,8,1,4,128]{4,1,3,2,0:T(8,128)S(1)} %copy.203), channel_id=1, source_target_pairs={{0,16},{1,17},{2,18},{3,19},{4,20},{5,21},{6,22},{7,23},{8,24},{9,... | collective-permute-start | bytes 393224 | tf_op jit(solution)/shard_map/ppermute | solution.py:21
  6.5 1.3 collective-permute-start
  7.8 0.9 bitcast_convert_fusion.53
  10.2 3.1 %collective-permute-done = f32[8,8,1,4,128]{4,1,3,2,0:T(8,128)S(1)} collective-permute-done((f32[8,8,1,4,128]{4,1,3,2,0:T(8,128)S(1)}, f32[8,8,1,4,128]{4,1,3,2,0:T(8,128)S(1)}, u32[]{:S(2)}, u32[]{:S(2)}) %collective-permute-start) | collective-permute-done | bytes 131104 | tf_op jit(solution)/shard_map/ppermute | solution.py:24
  13.4 1.3 collective-permute-start.2
  14.7 3.0 %collective-permute-start.3 = (f32[8,8,3,1,128]{4,1,3,2,0:T(8,128)S(1)}, f32[8,8,3,1,128]{4,1,3,2,0:T(8,128)S(1)}, u32[]{:S(2)}, u32[]{:S(2)}) collective-permute-start(f32[8,8,3,1,128]{4,1,3,2,0:T(8,128)S(1)} %get-tuple-element.285), channel_id=1, source_target_pairs={{0,4},{4,8},{8,12},{1,5},{5,9},{9,13},{2,6},{6,10},{10,14},{3,7},{... | collective-permute-start | bytes 294920 | tf_op jit(solution)/shard_map/ppermute | solution.py:21
  18.9 0.9 copy.278
  19.8 3.5 %collective-permute-start.5 = (f32[8,8,3,6,1]{1,0,4,3,2:T(8,128)S(1)}, f32[8,8,3,6,1]{1,0,4,3,2:T(8,128)S(1)}, u32[]{:S(2)}, u32[]{:S(2)}) collective-permute-start(f32[8,8,3,6,1]{1,0,4,3,2:T(8,128)S(1)} %copy.278), channel_id=1, source_target_pairs={{0,1},{1,2},{2,3},{4,5},{5,6},{6,7},{8,9},{9,10},{10,11},{12,13},{... | collective-permute-start | bytes 13832 | tf_op jit(solution)/shard_map/ppermute | solution.py:21
  24.2 1.3 collective-permute-start.4
  25.6 0.9 copy.209
  26.7 4.0 %collective-permute-done.4 = f32[8,8,3,6,1]{1,0,4,3,2:T(8,128)S(1)} collective-permute-done((f32[8,8,3,6,1]{1,0,4,3,2:T(8,128)S(1)}, f32[8,8,3,6,1]{1,0,4,3,2:T(8,128)S(1)}, u32[]{:S(2)}, u32[]{:S(2)}) %collective-permute-start.4) | collective-permute-done | bytes 4640 | tf_op jit(solution)/shard_map/ppermute | solution.py:24
  30.7 0.9 copy.207
  31.8 1.0 multiply_add_fusion.2
  33.6 41.6 %all-reduce.1 = (f32[8,8]{0,1:T(8,128)S(1)}, f32[8,8]{1,0:T(8,128)S(1)}, f32[8,8]{0,1:T(8,128)S(1)}) all-reduce(f32[8,8]{0,1:T(8,128)S(1)} %convolution_bitcast_fusion.13, f32[8,8]{1,0:T(8,128)S(1)} %convolution_bitcast_fusion.12, f32[8,8]{0,1:T(8,128)S(1)} %convolution_bitcast_fusion.11), channel_id=1, replica_groups=mesh['gx'=2,'gy'=4,'gz'=4] {'gx','gy','gz'}, use_global_device_ids=true, to_apply=%region_0.0 | all-reduce | flops 192 | bytes 1536 | tf_op jit(solution)/shard_map/psum | solution.py:71
  83.0 1.3 collective-permute-start.6
  84.3 4.6 %collective-permute-start.7 = (f32[8,8,1,4,128]{4,1,3,0,2:T(8,128)S(1)}, f32[8,8,1,4,128]{4,1,3,0,2:T(8,128)S(1)}, u32[]{:S(2)}, u32[]{:S(2)}) collective-permute-start(f32[8,8,1,4,128]{4,1,3,0,2:T(8,128)S(1)} %bitcast.788), channel_id=1, source_target_pairs={{0,16},{1,17},{2,18},{3,19},{4,20},{5,21},{6,22},{7,23},{8,24},{9,... | collective-permute-start | bytes 393224 | tf_op jit(solution)/shard_map/ppermute | solution.py:21
  90.8 2.8 and_reduce_fusion
  93.7 1.3 collective-permute-start.8
  95.0 3.0 %collective-permute-start.9 = (f32[8,8,3,1,128]{4,1,3,0,2:T(8,128)S(1)}, f32[8,8,3,1,128]{4,1,3,0,2:T(8,128)S(1)}, u32[]{:S(2)}, u32[]{:S(2)}) collective-permute-start(f32[8,8,3,1,128]{4,1,3,0,2:T(8,128)S(1)} %get-tuple-element.283), channel_id=1, source_target_pairs={{0,4},{4,8},{8,12},{1,5},{5,9},{9,13},{2,6},{6,10},{10,14},{3,7},{... | collective-permute-start | bytes 294920 | tf_op jit(solution)/shard_map/ppermute | solution.py:21
  99.2 0.9 copy.218
  100.1 2.2 collective-permute-start.11
  103.2 1.3 collective-permute-start.10
  104.6 0.9 copy.219
  105.7 3.7 %collective-permute-done.10 = f32[8,8,3,6,1]{1,0,4,3,2:T(8,128)S(1)} collective-permute-done((f32[8,8,3,6,1]{1,0,4,3,2:T(8,128)S(1)}, f32[8,8,3,6,1]{1,0,4,3,2:T(8,128)S(1)}, u32[]{:S(2)}, u32[]{:S(2)}) %collective-permute-start.10) | collective-permute-done | bytes 4640 | tf_op jit(solution)/shard_map/ppermute | solution.py:24
  109.4 0.9 copy.217
  110.6 1.1 multiply_add_fusion.1
  111.7 1.6 convolution_bitcast_fusion.7
  113.3 68.6 %all-gather = f32[96,8,8]{2,1,0:T(8,128)S(1)} all-gather(f32[3,8,8]{2,1,0:T(8,128)S(1)} %convolution_bitcast_fusion.7), channel_id=2, replica_groups=mesh['gx'=2,'gy'=4,'gz'=4] {'gx','gy','gz'}, dimensions={0}, use_global_device_ids=true | all-gather | bytes 25344 | tf_op jit(solution)/shard_map/all_gather | solution.py:12
  185.7 1.3 fusion.3
  187.2 1.3 collective-permute-start.12
  188.5 4.6 %collective-permute-start.13 = (f32[8,8,1,4,128]{4,1,3,0,2:T(8,128)S(1)}, f32[8,8,1,4,128]{4,1,3,0,2:T(8,128)S(1)}, u32[]{:S(2)}, u32[]{:S(2)}) collective-permute-start(f32[8,8,1,4,128]{4,1,3,0,2:T(8,128)S(1)} %bitcast.805), channel_id=1, source_target_pairs={{0,16},{1,17},{2,18},{3,19},{4,20},{5,21},{6,22},{7,23},{8,24},{9,... | collective-permute-start | bytes 393224 | tf_op jit(solution)/shard_map/ppermute | solution.py:21
  193.2 1.3 fusion.499
  194.5 1.1 collective-permute-done.13
  195.6 1.3 collective-permute-start.14
  196.9 3.0 %collective-permute-start.15 = (f32[8,8,3,1,128]{4,1,3,0,2:T(8,128)S(1)}, f32[8,8,3,1,128]{4,1,3,0,2:T(8,128)S(1)}, u32[]{:S(2)}, u32[]{:S(2)}) collective-permute-start(f32[8,8,3,1,128]{4,1,3,0,2:T(8,128)S(1)} %get-tuple-element.281), channel_id=1, source_target_pairs={{0,4},{4,8},{8,12},{1,5},{5,9},{9,13},{2,6},{6,10},{10,14},{3,7},{... | collective-permute-start | bytes 294920 | tf_op jit(solution)/shard_map/ppermute | solution.py:21
  201.1 0.9 copy.230
  202.0 2.3 collective-permute-start.17
  205.3 1.3 collective-permute-start.16
  206.7 0.9 copy.231
  207.9 3.9 %collective-permute-done.16 = f32[8,8,3,6,1]{1,0,4,3,2:T(8,128)S(1)} collective-permute-done((f32[8,8,3,6,1]{1,0,4,3,2:T(8,128)S(1)}, f32[8,8,3,6,1]{1,0,4,3,2:T(8,128)S(1)}, u32[]{:S(2)}, u32[]{:S(2)}) %collective-permute-start.16) | collective-permute-done | bytes 4640 | tf_op jit(solution)/shard_map/ppermute | solution.py:24
  211.8 0.9 copy.229
  213.0 1.0 multiply_add_fusion
  214.0 1.6 convolution_bitcast_fusion.6
  215.6 68.1 %all-gather.1 = f32[128,8,8]{2,1,0:T(8,128)S(1)} all-gather(f32[4,8,8]{2,1,0:T(8,128)S(1)} %convolution_bitcast_fusion.6), channel_id=3, replica_groups=mesh['gx'=2,'gy'=4,'gz'=4] {'gx','gy','gz'}, dimensions={0}, use_global_device_ids=true | all-gather | bytes 33792 | tf_op jit(solution)/shard_map/all_gather | solution.py:12
  288.1 1.1 fusion.7
  289.6 0.9 copy.245
  290.5 3.3 %fusion.498 = f32[4,8,3,8]{3,1,2,0:T(8,128)} fusion(f32[4,8,3,8]{3,1,2,0:T(8,128)} %copy-done.2, s32[]{:T(128)} %bitcast.381, s32[]{:T(128)} %bitcast.382, f32[4,8,8]{2,1,0:T(8,128)S(1)} %reduce_sum.19, pred[]{:T(512)} %get-tuple-element.118), kind=kLoop, calls=%fused_computation.797 | loop fusion | flops 64 | bytes 9984 | tf_op jit(solution)/shard_map/scatter | solution.py:99
  (151 shorter events, 30.3 us)
Async XLA Ops:
  0.6 8.1 %copy-start.1 = (bf16[7,8,8,1,4,128]{5,4,3,2,1,0:T(4,128)(2,1)S(1)}, bf16[7,8,8,1,4,128]{5,4,3,2,1,0:T(4,128)(2,1)}, u32[]{:S(2)}) copy-start(bf16[7,8,8,1,4,128]{5,4,3,2,1,0:T(4,128)(2,1)} %param.24) | copy-start | bytes 1376260
  1.6 8.5 %collective-permute-start.1 = (f32[8,8,1,4,128]{4,1,3,2,0:T(8,128)S(1)}, f32[8,8,1,4,128]{4,1,3,2,0:T(8,128)S(1)}, u32[]{:S(2)}, u32[]{:S(2)}) collective-permute-start(f32[8,8,1,4,128]{4,1,3,2,0:T(8,128)S(1)} %copy.203), channel_id=1, source_target_pairs={{0,16},{1,17},{2,18},{3,19},{4,20},{5,21},{6,22},{7,23},{8,24},{9,... | collective-permute-start | bytes 393224 | tf_op jit(solution)/shard_map/ppermute | solution.py:21
  6.5 6.9 %collective-permute-start = (f32[8,8,1,4,128]{4,1,3,2,0:T(8,128)S(1)}, f32[8,8,1,4,128]{4,1,3,2,0:T(8,128)S(1)}, u32[]{:S(2)}, u32[]{:S(2)}) collective-permute-start(f32[8,8,1,4,128]{4,1,3,2,0:T(8,128)S(1)} %copy.203), channel_id=1, source_target_pairs={{16,0},{17,1},{18,2},{19,3},{20,4},{21,5},{22,6},{23,7},{24,8},{25... | collective-permute-start | bytes 393224 | tf_op jit(solution)/shard_map/ppermute | solution.py:24
  8.8 0.9 copy-start
  13.4 4.4 %collective-permute-start.2 = (f32[8,8,3,1,128]{4,1,3,2,0:T(8,128)S(1)}, f32[8,8,3,1,128]{4,1,3,2,0:T(8,128)S(1)}, u32[]{:S(2)}, u32[]{:S(2)}) collective-permute-start(f32[8,8,3,1,128]{4,1,3,2,0:T(8,128)S(1)} %get-tuple-element.286), channel_id=1, source_target_pairs={{4,0},{8,4},{12,8},{5,1},{9,5},{13,9},{6,2},{10,6},{14,10},{7,3},{... | collective-permute-start | bytes 294920 | tf_op jit(solution)/shard_map/ppermute | solution.py:24
  14.7 4.0 %collective-permute-start.3 = (f32[8,8,3,1,128]{4,1,3,2,0:T(8,128)S(1)}, f32[8,8,3,1,128]{4,1,3,2,0:T(8,128)S(1)}, u32[]{:S(2)}, u32[]{:S(2)}) collective-permute-start(f32[8,8,3,1,128]{4,1,3,2,0:T(8,128)S(1)} %get-tuple-element.285), channel_id=1, source_target_pairs={{0,4},{4,8},{8,12},{1,5},{5,9},{9,13},{2,6},{6,10},{10,14},{3,7},{... | collective-permute-start | bytes 294920 | tf_op jit(solution)/shard_map/ppermute | solution.py:21
  19.8 5.7 %collective-permute-start.5 = (f32[8,8,3,6,1]{1,0,4,3,2:T(8,128)S(1)}, f32[8,8,3,6,1]{1,0,4,3,2:T(8,128)S(1)}, u32[]{:S(2)}, u32[]{:S(2)}) collective-permute-start(f32[8,8,3,6,1]{1,0,4,3,2:T(8,128)S(1)} %copy.278), channel_id=1, source_target_pairs={{0,1},{1,2},{2,3},{4,5},{5,6},{6,7},{8,9},{9,10},{10,11},{12,13},{... | collective-permute-start | bytes 13832 | tf_op jit(solution)/shard_map/ppermute | solution.py:21
  24.2 6.5 %collective-permute-start.4 = (f32[8,8,3,6,1]{1,0,4,3,2:T(8,128)S(1)}, f32[8,8,3,6,1]{1,0,4,3,2:T(8,128)S(1)}, u32[]{:S(2)}, u32[]{:S(2)}) collective-permute-start(f32[8,8,3,6,1]{1,0,4,3,2:T(8,128)S(1)} %copy.277), channel_id=1, source_target_pairs={{1,0},{2,1},{3,2},{5,4},{6,5},{7,6},{9,8},{10,9},{11,10},{13,12},{... | collective-permute-start | bytes 13832 | tf_op jit(solution)/shard_map/ppermute | solution.py:24
  83.0 10.6 %collective-permute-start.6 = (f32[8,8,1,4,128]{4,1,3,0,2:T(8,128)S(1)}, f32[8,8,1,4,128]{4,1,3,0,2:T(8,128)S(1)}, u32[]{:S(2)}, u32[]{:S(2)}) collective-permute-start(f32[8,8,1,4,128]{4,1,3,0,2:T(8,128)S(1)} %bitcast.787), channel_id=1, source_target_pairs={{16,0},{17,1},{18,2},{19,3},{20,4},{21,5},{22,6},{23,7},{24,8},{25... | collective-permute-start | bytes 393224 | tf_op jit(solution)/shard_map/ppermute | solution.py:24
  84.3 9.3 %collective-permute-start.7 = (f32[8,8,1,4,128]{4,1,3,0,2:T(8,128)S(1)}, f32[8,8,1,4,128]{4,1,3,0,2:T(8,128)S(1)}, u32[]{:S(2)}, u32[]{:S(2)}) collective-permute-start(f32[8,8,1,4,128]{4,1,3,0,2:T(8,128)S(1)} %bitcast.788), channel_id=1, source_target_pairs={{0,16},{1,17},{2,18},{3,19},{4,20},{5,21},{6,22},{7,23},{8,24},{9,... | collective-permute-start | bytes 393224 | tf_op jit(solution)/shard_map/ppermute | solution.py:21
  90.1 0.7 copy-start.3
  93.7 4.4 %collective-permute-start.8 = (f32[8,8,3,1,128]{4,1,3,0,2:T(8,128)S(1)}, f32[8,8,3,1,128]{4,1,3,0,2:T(8,128)S(1)}, u32[]{:S(2)}, u32[]{:S(2)}) collective-permute-start(f32[8,8,3,1,128]{4,1,3,0,2:T(8,128)S(1)} %get-tuple-element.284), channel_id=1, source_target_pairs={{4,0},{8,4},{12,8},{5,1},{9,5},{13,9},{6,2},{10,6},{14,10},{7,3},{... | collective-permute-start | bytes 294920 | tf_op jit(solution)/shard_map/ppermute | solution.py:24
  95.0 4.0 %collective-permute-start.9 = (f32[8,8,3,1,128]{4,1,3,0,2:T(8,128)S(1)}, f32[8,8,3,1,128]{4,1,3,0,2:T(8,128)S(1)}, u32[]{:S(2)}, u32[]{:S(2)}) collective-permute-start(f32[8,8,3,1,128]{4,1,3,0,2:T(8,128)S(1)} %get-tuple-element.283), channel_id=1, source_target_pairs={{0,4},{4,8},{8,12},{1,5},{5,9},{9,13},{2,6},{6,10},{10,14},{3,7},{... | collective-permute-start | bytes 294920 | tf_op jit(solution)/shard_map/ppermute | solution.py:21
  100.1 4.5 %collective-permute-start.11 = (f32[8,8,3,6,1]{1,0,4,3,2:T(8,128)S(1)}, f32[8,8,3,6,1]{1,0,4,3,2:T(8,128)S(1)}, u32[]{:S(2)}, u32[]{:S(2)}) collective-permute-start(f32[8,8,3,6,1]{1,0,4,3,2:T(8,128)S(1)} %copy.218), channel_id=1, source_target_pairs={{0,1},{1,2},{2,3},{4,5},{5,6},{6,7},{8,9},{9,10},{10,11},{12,13},{... | collective-permute-start | bytes 13832 | tf_op jit(solution)/shard_map/ppermute | solution.py:21
  103.2 6.2 %collective-permute-start.10 = (f32[8,8,3,6,1]{1,0,4,3,2:T(8,128)S(1)}, f32[8,8,3,6,1]{1,0,4,3,2:T(8,128)S(1)}, u32[]{:S(2)}, u32[]{:S(2)}) collective-permute-start(f32[8,8,3,6,1]{1,0,4,3,2:T(8,128)S(1)} %copy.216), channel_id=1, source_target_pairs={{1,0},{2,1},{3,2},{5,4},{6,5},{7,6},{9,8},{10,9},{11,10},{13,12},{... | collective-permute-start | bytes 13832 | tf_op jit(solution)/shard_map/ppermute | solution.py:24
  187.2 7.3 %collective-permute-start.12 = (f32[8,8,1,4,128]{4,1,3,0,2:T(8,128)S(1)}, f32[8,8,1,4,128]{4,1,3,0,2:T(8,128)S(1)}, u32[]{:S(2)}, u32[]{:S(2)}) collective-permute-start(f32[8,8,1,4,128]{4,1,3,0,2:T(8,128)S(1)} %bitcast.804), channel_id=1, source_target_pairs={{16,0},{17,1},{18,2},{19,3},{20,4},{21,5},{22,6},{23,7},{24,8},{25... | collective-permute-start | bytes 393224 | tf_op jit(solution)/shard_map/ppermute | solution.py:24
  188.5 7.1 %collective-permute-start.13 = (f32[8,8,1,4,128]{4,1,3,0,2:T(8,128)S(1)}, f32[8,8,1,4,128]{4,1,3,0,2:T(8,128)S(1)}, u32[]{:S(2)}, u32[]{:S(2)}) collective-permute-start(f32[8,8,1,4,128]{4,1,3,0,2:T(8,128)S(1)} %bitcast.805), channel_id=1, source_target_pairs={{0,16},{1,17},{2,18},{3,19},{4,20},{5,21},{6,22},{7,23},{8,24},{9,... | collective-permute-start | bytes 393224 | tf_op jit(solution)/shard_map/ppermute | solution.py:21
  195.6 4.4 %collective-permute-start.14 = (f32[8,8,3,1,128]{4,1,3,0,2:T(8,128)S(1)}, f32[8,8,3,1,128]{4,1,3,0,2:T(8,128)S(1)}, u32[]{:S(2)}, u32[]{:S(2)}) collective-permute-start(f32[8,8,3,1,128]{4,1,3,0,2:T(8,128)S(1)} %get-tuple-element.282), channel_id=1, source_target_pairs={{4,0},{8,4},{12,8},{5,1},{9,5},{13,9},{6,2},{10,6},{14,10},{7,3},{... | collective-permute-start | bytes 294920 | tf_op jit(solution)/shard_map/ppermute | solution.py:24
  196.9 4.0 %collective-permute-start.15 = (f32[8,8,3,1,128]{4,1,3,0,2:T(8,128)S(1)}, f32[8,8,3,1,128]{4,1,3,0,2:T(8,128)S(1)}, u32[]{:S(2)}, u32[]{:S(2)}) collective-permute-start(f32[8,8,3,1,128]{4,1,3,0,2:T(8,128)S(1)} %get-tuple-element.281), channel_id=1, source_target_pairs={{0,4},{4,8},{8,12},{1,5},{5,9},{9,13},{2,6},{6,10},{10,14},{3,7},{... | collective-permute-start | bytes 294920 | tf_op jit(solution)/shard_map/ppermute | solution.py:21
  200.0 0.9 copy-start.2
  202.0 4.7 %collective-permute-start.17 = (f32[8,8,3,6,1]{1,0,4,3,2:T(8,128)S(1)}, f32[8,8,3,6,1]{1,0,4,3,2:T(8,128)S(1)}, u32[]{:S(2)}, u32[]{:S(2)}) collective-permute-start(f32[8,8,3,6,1]{1,0,4,3,2:T(8,128)S(1)} %copy.230), channel_id=1, source_target_pairs={{0,1},{1,2},{2,3},{4,5},{5,6},{6,7},{8,9},{9,10},{10,11},{12,13},{... | collective-permute-start | bytes 13832 | tf_op jit(solution)/shard_map/ppermute | solution.py:21
  205.3 6.5 %collective-permute-start.16 = (f32[8,8,3,6,1]{1,0,4,3,2:T(8,128)S(1)}, f32[8,8,3,6,1]{1,0,4,3,2:T(8,128)S(1)}, u32[]{:S(2)}, u32[]{:S(2)}) collective-permute-start(f32[8,8,3,6,1]{1,0,4,3,2:T(8,128)S(1)} %copy.228), channel_id=1, source_target_pairs={{1,0},{2,1},{3,2},{5,4},{6,5},{7,6},{9,8},{10,9},{11,10},{13,12},{... | collective-permute-start | bytes 13832 | tf_op jit(solution)/shard_map/ppermute | solution.py:24
